TPU v7x, 32 devices: a whole 2x2x4 slice. The times are simulated.
32 devices in a mesh: dom: 4 (over z), col: 8 (over y, x, core).
Axes of the slice: x: 2, y: 2, z: 4, core: 2. Of those that a mesh axis runs over, the one named last changes fastest.
Arguments:
- rhs_interior: bfloat16 [4, 48, 8192], P('dom', 'col'), may hold values from -6 to 6
- interior_inv: bfloat16 [4, 8192, 8192], P('dom', None, 'col'), may hold values from -0.0625 to 0.0625
- coupling: bfloat16 [4, 8192, 768], P('dom', 'col'), may hold values from -0.0625 to 0.0625
- rhs_interface: bfloat16 [48, 8192], P('col', 'dom'), may hold values from -6 to 6
- block_ids: int32 [4, 6], P('dom'), may hold values from 0 to 63, as said below
- interface_inv: bfloat16 [8192, 8192], P('dom', 'col'), may hold values from -0.0625 to 0.0625
Outputs:
- interior_solution: bfloat16 [4, 48, 8192], P('dom', None, 'col')
- interface_solution: bfloat16 [48, 8192], P('col')
Inputs may be any that keep to these rules, and one draw needn't show every extreme that they name: `block_ids`: each row names 6 different blocks.
All inputs are finite; a program needn't handle non-finite values.
Results may differ from a plain program's by a relative error of at most 0.025.
Values may be sent and summed in bfloat16 or wider, within the bound.
No kernel may reach another device: no remote copies, remote signals or barrier semaphores. Data moves between devices by JAX's collectives and lax.ppermute only.
A program may use at most 64 MiB of HBM per device.

v0:
```python
import jax
import jax.numpy as jnp
from jax import lax
from jax.sharding import PartitionSpec as P

G = 8192
BS = 128


def per_device(rhs_interior, interior_inv, coupling, rhs_interface, block_ids, interface_inv):
    rhs_local = rhs_interior[0]
    inverse = interior_inv[0]
    couple = coupling[0]
    blocks = block_ids[0]
    row_count = rhs_local.shape[0]
    block_count = blocks.shape[0]
    nblocks = G // BS
    onehot = (blocks[:, None] == jnp.arange(nblocks, dtype=jnp.int32)[None, :]).astype(jnp.float32)
    interior_step = jnp.dot(
        lax.all_gather(rhs_local, "col", axis=0, tiled=True),
        inverse,
        preferred_element_type=jnp.float32,
    ).astype(jnp.bfloat16)
    contribution = lax.psum_scatter(
        jnp.dot(interior_step, couple, preferred_element_type=jnp.float32).astype(jnp.bfloat16),
        "col",
        scatter_dimension=0,
        tiled=True,
    ).astype(jnp.float32)
    placed = jnp.einsum(
        "kb,rks->rbs", onehot, contribution.reshape(row_count, block_count, BS)
    ).reshape(row_count, G)
    summed = lax.psum_scatter(
        placed.astype(jnp.bfloat16), "dom", scatter_dimension=1, tiled=True
    ).astype(jnp.float32)
    reduced = (rhs_interface.astype(jnp.float32) - summed).astype(jnp.bfloat16)
    partial_solution = jnp.dot(
        lax.all_gather(reduced, "col", axis=0, tiled=True),
        interface_inv,
        preferred_element_type=jnp.float32,
    )
    column_total = lax.psum(partial_solution.astype(jnp.bfloat16), "dom")
    solution = lax.all_to_all(column_total, "col", split_axis=0, concat_axis=1, tiled=True)
    local_solution = jnp.einsum(
        "kb,rbs->rks",
        onehot.astype(jnp.bfloat16),
        solution.reshape(row_count, nblocks, BS),
        preferred_element_type=jnp.float32,
    )
    local_solution = local_solution.reshape(row_count, block_count * BS).astype(jnp.bfloat16)
    every_solution = lax.all_gather(local_solution, "col", axis=0, tiled=True)
    correction = jnp.einsum("rl,il->ri", every_solution, couple, preferred_element_type=jnp.float32)
    rhs_columns = lax.all_to_all(rhs_local, "col", split_axis=1, concat_axis=0, tiled=True)
    interior_rhs = (rhs_columns.astype(jnp.float32) - correction).astype(jnp.bfloat16)
    result = jnp.dot(
        lax.all_gather(interior_rhs, "col", axis=1, tiled=True),
        inverse,
        preferred_element_type=jnp.float32,
    )
    interior_solution = result.astype(jnp.bfloat16)[None]
    return (interior_solution, solution)


def solution(mesh):
    placed = (
        P("dom", "col", None),
        P("dom", None, "col"),
        P("dom", "col", None),
        P("col", "dom"),
        P("dom", None),
        P("dom", "col"),
    )
    return jax.shard_map(
        per_device,
        mesh=mesh,
        in_specs=placed,
        out_specs=(P("dom", None, "col"), P("col", None)),
        check_vma=False,
    )
```

profile of v0, /device:TPU:0, one launch (start us, length us, event | category | flops | bytes accessed | tf_op | source)
XLA Modules:
  0.0 168.0 jit_solution(9237124908893844768)
XLA Ops:
  7.2 0.0 copy-start
  7.2 0.0 reduce-scatter.4.cloned.1.call-start
  7.2 1.2 copy.15
  8.4 14.6 %all-gather = bf16[1,48,8192]{2,0,1:T(2,128)(2,1)S(1)} all-gather(bf16[1,6,8192]{2,0,1:T(2,128)(2,1)S(1)} %copy.15), channel_id=2, replica_groups=mesh['dom'=4,'col'=8] {'col'}, dimensions={1}, use_global_device_ids=true | all-gather | bytes 884736 | tf_op jit(solution)/shard_map/all_gather | solution.py:20
  23.0 0.0 copy-done
  23.0 0.0 copy-start.3
  23.0 0.0 copy-start.4
  23.0 0.0 copy-start.2
  23.0 9.5 %fusion.21 = bf16[48,768]{1,0:T(8,128)(2,1)S(1)} fusion(bf16[1,1024,768]{2,1,0:T(8,128)(2,1)S(1)} %copy-done, bf16[1,8192,1024]{2,1,0:T(8,128)(2,1)} %param.7, bf16[1,48,8192]{2,0,1:T(2,128)(2,1)S(1)} %all-gather), kind=kOutput, calls=%fused_computation.14 | convolution fusion | flops 880889856 | bytes 19210240 | tf_op jit(solution)/shard_map/dot_general | solution.py:25
  32.6 0.0 copy-start.1
  32.6 14.5 %fusion = bf16[8,768]{1,0:T(8,128)(2,1)S(1)} fusion(bf16[48,768]{1,0:T(8,128)(2,1)S(1)} %fusion.21), kind=kCustom, calls=%all-reduce-scatter | all-reduce-scatter fusion | flops 49153 | bytes 86528
  47.1 1.3 collective-permute-start
  48.4 2.0 %collective-permute-start.1 = (bf16[6,768]{1,0:T(8,128)(2,1)S(1)}, bf16[6,768]{1,0:T(8,128)(2,1)S(1)}, u32[]{:S(2)}, u32[]{:S(2)}) collective-permute-start(bf16[6,768]{1,0:T(8,128)(2,1)S(1)} %slice), channel_id=1, source_target_pairs={{0,2},{1,3},{2,4},{3,5},{4,6},{5,7},{8,10},{9,11},{10,12},{11,13},... | collective-permute-start | bytes 27656
  50.4 0.0 copy-done.3
  50.4 0.6 dynamic-slice.4
  51.7 0.1 collective-permute-done.1
  51.8 0.0 collective-permute-done
  51.8 0.2 concatenate
  52.1 0.0 copy-done.4
  52.1 0.3 fusion.24
  52.4 0.7 copy.25
  53.1 0.0 reduce-scatter.4.cloned.1.call-update
  53.1 0.0 all-reduce.4.cloned.1.call-start
  53.2 23.2 %reduce-scatter.4.cloned.1.call-done = bf16[6,2048]{1,0:T(8,128)(2,1)} async-done(((bf16[6,8192]{1,0:T(8,128)(2,1)}), bf16[6,2048]{1,0:T(8,128)(2,1)}) %reduce-scatter.4.cloned.1.call-update) | async-done | bytes 24592 | tf_op jit(solution)/shard_map/reduce_scatter | solution.py:33
  76.4 0.0 copy-done.2
  76.4 0.8 fusion.35
  77.1 9.3 %all-gather.1 = bf16[8,6,2048]{2,1,0:T(8,128)(2,1)S(1)} all-gather(bf16[1,6,2048]{2,1,0:T(8,128)(2,1)S(1)} %fusion.35), channel_id=1, replica_groups=mesh['dom'=4,'col'=8] {'col'}, dimensions={0}, use_global_device_ids=true | all-gather | bytes 221184 | tf_op jit(solution)/shard_map/all_gather | solution.py:38
  86.4 0.1 reshape.30
  86.5 3.0 %convolution_convert_fusion = bf16[48,1024]{1,0:T(8,128)(2,1)S(1)} fusion(bf16[48,2048]{1,0:T(8,128)(2,1)S(1)} %reshape.30, bf16[2048,1024]{1,0:T(8,128)(2,1)} %param.11), kind=kOutput, calls=%fused_computation.12 | convolution fusion | flops 201375744 | bytes 4489216 | tf_op jit(solution)/shard_map/dot_general | solution.py:37
  89.5 0.7 all_to_all.26
  90.2 0.0 all-reduce.4.cloned.1.call-update
  90.2 0.0 copy-done.1
  90.2 8.0 %all_to_all.32 = bf16[6,8,1024]{2,0,1:T(8,128)(2,1)S(1)} all-to-all(bf16[6,8,1024]{2,0,1:T(8,128)(2,1)S(1)} %bitcast.65), channel_id=1, replica_groups=mesh['dom'=4,'col'=8] {'col'}, dimensions={1} | all-to-all | bytes 196608 | tf_op jit(solution)/shard_map/all_to_all | solution.py:53
  98.3 24.0 %all-reduce.4.cloned.1.call-done = bf16[8,6,1024]{2,1,0:T(8,128)(2,1)} async-done(((bf16[8,6,1024]{2,1,0:T(8,128)(2,1)}), bf16[8,6,1024]{2,1,0:T(8,128)(2,1)}) %all-reduce.4.cloned.1.call-update) | async-done | bytes 98320 | tf_op jit(solution)/shard_map/psum | solution.py:42
  122.3 3.6 %all-to-all-start.1 = ((bf16[8,6,1024]{2,1,0:T(8,128)(2,1)}), bf16[8,6,1024]{2,1,0:T(8,128)(2,1)S(1)}, u32[]{:S(2)}, u32[]{:S(2)}) async-start(bf16[8,6,1024]{2,1,0:T(8,128)(2,1)} %all-reduce.4.cloned.1.call-done), calls=%async_computation.2 | async-start | bytes 262144 | tf_op jit(solution)/shard_map/all_to_all | solution.py:43
  126.0 5.4 %all-to-all-done.1 = bf16[8,6,1024]{2,1,0:T(8,128)(2,1)S(1)} async-done(((bf16[8,6,1024]{2,1,0:T(8,128)(2,1)}), bf16[8,6,1024]{2,1,0:T(8,128)(2,1)S(1)}, u32[]{:S(2)}, u32[]{:S(2)}) %all-to-all-start.1) | async-done | bytes 98336 | tf_op jit(solution)/shard_map/all_to_all | solution.py:43
  131.4 0.1 copy.16
  131.5 0.2 fusion.28
  131.7 8.3 %all-gather.2 = bf16[8,6,768]{2,1,0:T(8,128)(2,1)S(1)} all-gather(bf16[1,6,768]{2,1,0:T(8,128)(2,1)S(1)} %reshape.31), channel_id=1, replica_groups=mesh['dom'=4,'col'=8] {'col'}, dimensions={0}, use_global_device_ids=true | all-gather | bytes 82944 | tf_op jit(solution)/shard_map/all_gather | solution.py:51
  140.1 0.6 fusion.12
  140.6 10.4 %all_gather.15 = bf16[48,8192]{1,0:T(8,128)(2,1)S(1)} all-gather(bf16[48,1024]{1,0:T(8,128)(2,1)S(1)} %fusion.12), channel_id=1, replica_groups=mesh['dom'=4,'col'=8] {'col'}, dimensions={1}, use_global_device_ids=true | all-gather | bytes 884736 | tf_op jit(solution)/shard_map/all_gather | solution.py:56
  151.0 9.5 %fusion.25 = bf16[1,48,1024]{2,1,0:T(8,128)(2,1)} fusion(bf16[48,8192]{1,0:T(8,128)(2,1)S(1)} %all_gather.15, bf16[1,8192,1024]{2,1,0:T(8,128)(2,1)} %param.7), kind=kOutput, calls=%fused_computation.16 | convolution fusion | flops 805355520 | bytes 17661952 | tf_op jit(solution)/shard_map/dot_general | solution.py:55
  160.5 0.7 copy.28
  (8 shorter events, 0.2 us)
Async XLA Ops:
  7.2 15.9 %copy-start = (bf16[1,1024,768]{2,1,0:T(8,128)(2,1)S(1)}, bf16[1,1024,768]{2,1,0:T(8,128)(2,1)}, u32[]{:S(2)}) copy-start(bf16[1,1024,768]{2,1,0:T(8,128)(2,1)} %param.8) | copy-start | bytes 4718596
  7.2 69.2 %reduce-scatter.4.cloned.1.call-start = ((), (), s32[]{:S(2)}) async-start(), calls=%async_computation.3 | async-start | bytes 163840 | tf_op jit(solution)/shard_map/reduce_scatter | solution.py:33
  23.0 27.4 %copy-start.3 = (u32[32]{0:T(128)S(1)}, u32[32]{0:T(128)}, u32[]{:S(2)}) copy-start(u32[32]{0:T(128)} %constant.7) | copy-start | bytes 388
  23.0 29.0 %copy-start.4 = (s32[1,6]{1,0:T(1,128)S(1)}, s32[1,6]{1,0:T(1,128)}, u32[]{:S(2)}) copy-start(s32[1,6]{1,0:T(1,128)} %param.10) | copy-start | bytes 76
  23.0 53.3 %copy-start.2 = (bf16[6,2048]{1,0:T(8,128)(2,1)S(1)}, bf16[6,2048]{1,0:T(8,128)(2,1)}, u32[]{:S(2)}) copy-start(bf16[6,2048]{1,0:T(8,128)(2,1)} %param.9) | copy-start | bytes 73732
  32.6 57.6 %copy-start.1 = (bf16[1,6,8192]{2,1,0:T(8,128)(2,1)S(1)}, bf16[1,6,8192]{2,1,0:T(8,128)(2,1)}, u32[]{:S(2)}) copy-start(bf16[1,6,8192]{2,1,0:T(8,128)(2,1)} %param.6) | copy-start | bytes 294916
  47.1 4.7 %collective-permute-start = (bf16[8,768]{1,0:T(8,128)(2,1)S(1)}, bf16[8,768]{1,0:T(8,128)(2,1)S(1)}, u32[]{:S(2)}, u32[]{:S(2)}) collective-permute-start(bf16[8,768]{1,0:T(8,128)(2,1)S(1)} %fusion), channel_id=1, source_target_pairs={{0,1},{1,2},{2,3},{3,4},{4,5},{5,6},{6,7},{8,9},{9,10},{10,11},{11... | collective-permute-start | bytes 36872
  48.4 3.4 %collective-permute-start.1 = (bf16[6,768]{1,0:T(8,128)(2,1)S(1)}, bf16[6,768]{1,0:T(8,128)(2,1)S(1)}, u32[]{:S(2)}, u32[]{:S(2)}) collective-permute-start(bf16[6,768]{1,0:T(8,128)(2,1)S(1)} %slice), channel_id=1, source_target_pairs={{0,2},{1,3},{2,4},{3,5},{4,6},{5,7},{8,10},{9,11},{10,12},{11,13},... | collective-permute-start | bytes 27656
  53.1 69.1 %all-reduce.4.cloned.1.call-start = ((), (), s32[]{:S(2)}) async-start(), calls=%async_computation.4 | async-start | bytes 262144 | tf_op jit(solution)/shard_map/psum | solution.py:42
  122.3 9.1 %all-to-all-start.1 = ((bf16[8,6,1024]{2,1,0:T(8,128)(2,1)}), bf16[8,6,1024]{2,1,0:T(8,128)(2,1)S(1)}, u32[]{:S(2)}, u32[]{:S(2)}) async-start(bf16[8,6,1024]{2,1,0:T(8,128)(2,1)} %all-reduce.4.cloned.1.call-done), calls=%async_computation.2 | async-start | bytes 262144 | tf_op jit(solution)/shard_map/all_to_all | solution.py:43
Sparse Core Ops, SparseCore 0:
  53.3 23.0 reduce-scatter.3
  90.3 31.8 all-reduce.3
where the time goes:
time: 169 us; the launch traced here: 168 us
  blocking collectives  65 us (38%)
  waiting for transfers between devices  52.8 us (31%)
  matrix products  23.1 us (14%)
  between operations  14.9 us (9%)
  starting transfers between devices  7.03 us (4%)
  local copies, waits for them, and re-layouts  4.39 us (3%)
    psum x1, waiting for transfers between devices, per_device(): column_total = lax.psum(partial_solution.astype(jnp.bfloat16), 'dom')  24 us
    reduce_scatter x1, waiting for transfers between devices, per_device(): lax.psum_scatter(placed.astype(jnp.bfloat16), 'dom', scatter_dimension=1,...  23.2 us
    all_gather x1, blocking collectives, per_device(): lax.all_gather(rhs_local, 'col', axis=0, tiled=True)  14.6 us
    unnamed x1, blocking collectives  14.5 us
    all_gather x1, blocking collectives, per_device(): lax.all_gather(interior_rhs, 'col', axis=1, tiled=True)  10.4 us
    dot_general x1, matrix products, per_device(): jnp.dot(interior_step, couple, preferred_element_type=jnp.float32)  9.54 us
    dot_general x1, matrix products, per_device(): jnp.dot(lax.all_gather(interior_rhs, 'col', axis=1, tiled=True), inverse,...  9.46 us
    all_gather x1, blocking collectives, per_device(): lax.all_gather(reduced, 'col', axis=0, tiled=True)  9.25 us
  transfers between devices with their start and end apart: 5, of which 4 were waited for; matrix products, arithmetic and copies ran while one was open for 0% of the time, Pallas kernels for 0%

commit v1 on v0

--- a/solution.py
+++ b/solution.py
@@ -5,6 +5,12 @@
 
 G = 8192
 BS = 128
+
+
+def stacked_exchange(block, axis, split, join):
+    pieces = jnp.split(block, lax.axis_size(axis), axis=split)
+    incoming = lax.all_to_all(jnp.stack(pieces), axis, 0, 0)
+    return jnp.concatenate(incoming, axis=join)
 
 
 def per_device(rhs_interior, interior_inv, coupling, rhs_interface, block_ids, interface_inv):
@@ -40,7 +46,7 @@
         preferred_element_type=jnp.float32,
     )
     column_total = lax.psum(partial_solution.astype(jnp.bfloat16), "dom")
-    solution = lax.all_to_all(column_total, "col", split_axis=0, concat_axis=1, tiled=True)
+    solution = stacked_exchange(column_total, "col", 0, 1)
     local_solution = jnp.einsum(
         "kb,rbs->rks",
         onehot.astype(jnp.bfloat16),

time: 169 us -> 179 us (1.059)
  local copies, waits for them, and re-layouts: 4.39 us -> 14.5 us
  blocking collectives: 65 us -> 56.9 us
  waiting for transfers between devices: 52.8 us -> 57.2 us
  starting transfers between devices: 7.03 us -> 10.4 us
    unnamed x20 -> x25, local copies, waits for them, and re-layouts: 3.53 us -> 13 us
    all_to_all x1 -> x0, blocking collectives: 8.04 us -> none  [per_device(): lax.all_to_all(rhs_local, 'col', split_axis=1, concat_axis=0, tiled=True)]
    psum x1, waiting for transfers between devices: 24 us -> 28.5 us  [per_device(): column_total = lax.psum(partial_solution.astype(jnp.bfloat16), 'dom')]
    all_to_all x1 -> x2, starting transfers between devices: 3.64 us -> 7.04 us  [the longest x1 3.66 us: stacked_exchange(): incoming = lax.all_to_all(jnp.stack(pieces), axis, 0, 0)]
    all_to_all x1 -> x2, waiting for transfers between devices: 5.44 us -> 5.44 us  [the longest x1 5.44 us: stacked_exchange(): incoming = lax.all_to_all(jnp.stack(pieces), axis, 0, 0)]
  transfers between devices with their start and end apart: 5 -> 6, of which waited for: 4 -> 4; matrix products, arithmetic and copies ran while one was open for 0% -> 6% of each run, Pallas kernels for 0% -> 0%
where the time goes in v1:
time: 179 us; the launch traced here: 178 us
  waiting for transfers between devices  57.2 us (32%)
  blocking collectives  56.9 us (32%)
  matrix products  23.7 us (13%)
  between operations  14.8 us (8%)
  local copies, waits for them, and re-layouts  14.5 us (8%)
  starting transfers between devices  10.4 us (6%)
    psum x1, waiting for transfers between devices, per_device(): column_total = lax.psum(partial_solution.astype(jnp.bfloat16), 'dom')  28.5 us
    reduce_scatter x1, waiting for transfers between devices, per_device(): lax.psum_scatter(placed.astype(jnp.bfloat16), 'dom', scatter_dimension=1,...  23.2 us
    all_gather x1, blocking collectives, per_device(): lax.all_gather(rhs_local, 'col', axis=0, tiled=True)  14.6 us
    unnamed x1, blocking collectives  14.3 us
    unnamed x25, local copies, waits for them, and re-layouts  13 us
    all_gather x1, blocking collectives, per_device(): lax.all_gather(interior_rhs, 'col', axis=1, tiled=True)  10.4 us
    dot_general x1, matrix products, per_device(): jnp.dot(interior_step, couple, preferred_element_type=jnp.float32)  9.54 us
    dot_general x1, matrix products, per_device(): jnp.dot(lax.all_gather(interior_rhs, 'col', axis=1, tiled=True), inverse,...  9.46 us
  transfers between devices with their start and end apart: 6, of which 4 were waited for; matrix products, arithmetic and copies ran while one was open for 6% of the time, Pallas kernels for 0%

profile of v1, /device:TPU:0, one launch (start us, length us, event | category | flops | bytes accessed | tf_op | source)
XLA Modules:
  0.0 178.4 jit_solution(11070030512985838979)
XLA Ops:
  7.2 0.0 copy-start
  7.2 0.0 reduce-scatter.4.cloned.1.call-start
  7.2 1.2 copy.14
  8.4 14.6 %all-gather = bf16[1,48,8192]{2,0,1:T(2,128)(2,1)S(1)} all-gather(bf16[1,6,8192]{2,0,1:T(2,128)(2,1)S(1)} %copy.14), channel_id=2, replica_groups=mesh['dom'=4,'col'=8] {'col'}, dimensions={1}, use_global_device_ids=true | all-gather | bytes 884736 | tf_op jit(solution)/shard_map/all_gather | solution.py:26
  23.0 0.0 copy-done
  23.0 0.0 copy-start.2
  23.0 0.0 copy-start.3
  23.0 9.5 %fusion.21 = bf16[48,768]{1,0:T(8,128)(2,1)S(1)} fusion(bf16[1,1024,768]{2,1,0:T(8,128)(2,1)S(1)} %copy-done, bf16[1,8192,1024]{2,1,0:T(8,128)(2,1)} %param.7, bf16[1,48,8192]{2,0,1:T(2,128)(2,1)S(1)} %all-gather), kind=kOutput, calls=%fused_computation.14 | convolution fusion | flops 880889856 | bytes 19210240 | tf_op jit(solution)/shard_map/dot_general | solution.py:31
  32.6 14.3 %fusion = bf16[8,768]{1,0:T(8,128)(2,1)S(1)} fusion(bf16[48,768]{1,0:T(8,128)(2,1)S(1)} %fusion.21), kind=kCustom, calls=%all-reduce-scatter | all-reduce-scatter fusion | flops 49153 | bytes 86528
  46.9 1.3 collective-permute-start
  48.2 2.0 %collective-permute-start.1 = (bf16[6,768]{1,0:T(8,128)(2,1)S(1)}, bf16[6,768]{1,0:T(8,128)(2,1)S(1)}, u32[]{:S(2)}, u32[]{:S(2)}) collective-permute-start(bf16[6,768]{1,0:T(8,128)(2,1)S(1)} %slice), channel_id=1, source_target_pairs={{0,2},{1,3},{2,4},{3,5},{4,6},{5,7},{8,10},{9,11},{10,12},{11,13},... | collective-permute-start | bytes 27656
  50.3 0.0 copy-done.2
  50.3 0.6 dynamic-slice.4
  51.5 0.1 collective-permute-done.1
  51.7 0.0 collective-permute-done
  51.7 0.2 concatenate
  51.9 0.0 copy-done.3
  51.9 0.3 fusion.24
  52.2 0.7 copy.24
  53.0 0.0 reduce-scatter.4.cloned.1.call-update
  53.0 0.0 all-reduce.4.cloned.1.call-start
  53.0 23.2 %reduce-scatter.4.cloned.1.call-done = bf16[6,2048]{1,0:T(8,128)(2,1)} async-done(((bf16[6,8192]{1,0:T(8,128)(2,1)}), bf16[6,2048]{1,0:T(8,128)(2,1)}) %reduce-scatter.4.cloned.1.call-update) | async-done | bytes 24592 | tf_op jit(solution)/shard_map/reduce_scatter | solution.py:39
  76.2 0.0 copy-done.1
  76.2 0.8 fusion.35
  77.0 9.3 %all-gather.1 = bf16[8,6,2048]{2,1,0:T(8,128)(2,1)S(1)} all-gather(bf16[1,6,2048]{2,1,0:T(8,128)(2,1)S(1)} %fusion.35), channel_id=1, replica_groups=mesh['dom'=4,'col'=8] {'col'}, dimensions={0}, use_global_device_ids=true | all-gather | bytes 221184 | tf_op jit(solution)/shard_map/all_gather | solution.py:44
  86.2 0.1 reshape.30
  86.3 3.7 %convolution_convert_fusion = bf16[48,1024]{1,0:T(8,128)(2,1)} fusion(bf16[48,2048]{1,0:T(8,128)(2,1)S(1)} %reshape.30, bf16[2048,1024]{1,0:T(8,128)(2,1)} %param.11), kind=kOutput, calls=%fused_computation.12 | convolution fusion | flops 201375744 | bytes 4489216 | tf_op jit(solution)/shard_map/dot_general | solution.py:43
  90.0 0.0 all-reduce.4.cloned.1.call-update
  90.0 3.4 %all-to-all-start = ((bf16[6,8,1024]{2,0,1:T(8,128)(2,1)}), bf16[6,8,1024]{2,0,1:T(8,128)(2,1)S(1)}, u32[]{:S(2)}, u32[]{:S(2)}) async-start(bf16[6,8,1024]{2,0,1:T(8,128)(2,1)} %bitcast), calls=%async_computation | async-start | bytes 262144 | tf_op jit(solution)/shard_map/all_to_all | solution.py:59
  93.4 28.5 %all-reduce.4.cloned.1.call-done = bf16[48,1024]{1,0:T(8,128)(2,1)} async-done(((bf16[48,1024]{1,0:T(8,128)(2,1)}), bf16[48,1024]{1,0:T(8,128)(2,1)}) %all-reduce.4.cloned.1.call-update) | async-done | bytes 98320 | tf_op jit(solution)/shard_map/psum | solution.py:48
  121.9 1.3 constant_dynamic-update-slice_fusion.7
  123.2 1.4 constant_dynamic-update-slice_fusion.6
  124.6 1.4 constant_dynamic-update-slice_fusion.5
  125.9 1.3 constant_dynamic-update-slice_fusion.4
  127.3 1.3 constant_dynamic-update-slice_fusion.3
  128.6 1.4 constant_dynamic-update-slice_fusion.2
  129.9 1.4 constant_dynamic-update-slice_fusion.1
  131.3 1.3 constant_dynamic-update-slice_fusion
  132.6 0.0 all-to-all-done
  132.7 3.7 %all-to-all-start.1 = ((bf16[8,6,1024]{2,1,0:T(8,128)(2,1)}), bf16[8,6,1024]{2,1,0:T(8,128)(2,1)S(1)}, u32[]{:S(2)}, u32[]{:S(2)}) async-start(bf16[8,6,1024]{2,1,0:T(8,128)(2,1)} %constant_dynamic-update-slice_fusion), calls=%async_computation.2 | async-start | bytes 262144 | tf_op jit(solution)/shard_map/all_to_all | solution.py:12
  136.4 5.4 %all-to-all-done.1 = bf16[8,6,1024]{2,1,0:T(8,128)(2,1)S(1)} async-done(((bf16[8,6,1024]{2,1,0:T(8,128)(2,1)}), bf16[8,6,1024]{2,1,0:T(8,128)(2,1)S(1)}, u32[]{:S(2)}, u32[]{:S(2)}) %all-to-all-start.1) | async-done | bytes 98336 | tf_op jit(solution)/shard_map/all_to_all | solution.py:12
  141.8 0.1 copy.15
  141.9 0.2 fusion.28
  142.2 8.3 %all-gather.2 = bf16[8,6,768]{2,1,0:T(8,128)(2,1)S(1)} all-gather(bf16[1,6,768]{2,1,0:T(8,128)(2,1)S(1)} %reshape.31), channel_id=1, replica_groups=mesh['dom'=4,'col'=8] {'col'}, dimensions={0}, use_global_device_ids=true | all-gather | bytes 82944 | tf_op jit(solution)/shard_map/all_gather | solution.py:57
  150.5 0.6 fusion.12
  151.1 10.4 %all_gather.15 = bf16[48,8192]{1,0:T(8,128)(2,1)S(1)} all-gather(bf16[48,1024]{1,0:T(8,128)(2,1)S(1)} %fusion.12), channel_id=1, replica_groups=mesh['dom'=4,'col'=8] {'col'}, dimensions={1}, use_global_device_ids=true | all-gather | bytes 884736 | tf_op jit(solution)/shard_map/all_gather | solution.py:62
  161.4 9.5 %fusion.25 = bf16[1,48,1024]{2,1,0:T(8,128)(2,1)} fusion(bf16[48,8192]{1,0:T(8,128)(2,1)S(1)} %all_gather.15, bf16[1,8192,1024]{2,1,0:T(8,128)(2,1)} %param.7), kind=kOutput, calls=%fused_computation.16 | convolution fusion | flops 805355520 | bytes 17661952 | tf_op jit(solution)/shard_map/dot_general | solution.py:61
  170.9 0.7 copy.34
  (9 shorter events, 0.2 us)
Async XLA Ops:
  7.2 15.9 %copy-start = (bf16[1,1024,768]{2,1,0:T(8,128)(2,1)S(1)}, bf16[1,1024,768]{2,1,0:T(8,128)(2,1)}, u32[]{:S(2)}) copy-start(bf16[1,1024,768]{2,1,0:T(8,128)(2,1)} %param.8) | copy-start | bytes 4718596
  7.2 69.0 %reduce-scatter.4.cloned.1.call-start = ((), (), s32[]{:S(2)}) async-start(), calls=%async_computation.3 | async-start | bytes 163840 | tf_op jit(solution)/shard_map/reduce_scatter | solution.py:39
  23.0 27.2 %copy-start.2 = (u32[32]{0:T(128)S(1)}, u32[32]{0:T(128)}, u32[]{:S(2)}) copy-start(u32[32]{0:T(128)} %constant.7) | copy-start | bytes 388
  23.0 28.9 %copy-start.3 = (s32[1,6]{1,0:T(1,128)S(1)}, s32[1,6]{1,0:T(1,128)}, u32[]{:S(2)}) copy-start(s32[1,6]{1,0:T(1,128)} %param.10) | copy-start | bytes 76
  23.0 53.2 %copy-start.1 = (bf16[6,2048]{1,0:T(8,128)(2,1)S(1)}, bf16[6,2048]{1,0:T(8,128)(2,1)}, u32[]{:S(2)}) copy-start(bf16[6,2048]{1,0:T(8,128)(2,1)} %param.9) | copy-start | bytes 73732
  46.9 4.7 %collective-permute-start = (bf16[8,768]{1,0:T(8,128)(2,1)S(1)}, bf16[8,768]{1,0:T(8,128)(2,1)S(1)}, u32[]{:S(2)}, u32[]{:S(2)}) collective-permute-start(bf16[8,768]{1,0:T(8,128)(2,1)S(1)} %fusion), channel_id=1, source_target_pairs={{0,1},{1,2},{2,3},{3,4},{4,5},{5,6},{6,7},{8,9},{9,10},{10,11},{11... | collective-permute-start | bytes 36872
  48.2 3.4 %collective-permute-start.1 = (bf16[6,768]{1,0:T(8,128)(2,1)S(1)}, bf16[6,768]{1,0:T(8,128)(2,1)S(1)}, u32[]{:S(2)}, u32[]{:S(2)}) collective-permute-start(bf16[6,768]{1,0:T(8,128)(2,1)S(1)} %slice), channel_id=1, source_target_pairs={{0,2},{1,3},{2,4},{3,5},{4,6},{5,7},{8,10},{9,11},{10,12},{11,13},... | collective-permute-start | bytes 27656
  53.0 68.9 %all-reduce.4.cloned.1.call-start = ((), (), s32[]{:S(2)}) async-start(), calls=%async_computation.4 | async-start | bytes 196608 | tf_op jit(solution)/shard_map/psum | solution.py:48
  90.0 42.6 %all-to-all-start = ((bf16[6,8,1024]{2,0,1:T(8,128)(2,1)}), bf16[6,8,1024]{2,0,1:T(8,128)(2,1)S(1)}, u32[]{:S(2)}, u32[]{:S(2)}) async-start(bf16[6,8,1024]{2,0,1:T(8,128)(2,1)} %bitcast), calls=%async_computation | async-start | bytes 262144 | tf_op jit(solution)/shard_map/all_to_all | solution.py:59
  132.7 9.2 %all-to-all-start.1 = ((bf16[8,6,1024]{2,1,0:T(8,128)(2,1)}), bf16[8,6,1024]{2,1,0:T(8,128)(2,1)S(1)}, u32[]{:S(2)}, u32[]{:S(2)}) async-start(bf16[8,6,1024]{2,1,0:T(8,128)(2,1)} %constant_dynamic-update-slice_fusion), calls=%async_computation.2 | async-start | bytes 262144 | tf_op jit(solution)/shard_map/all_to_all | solution.py:12
Sparse Core Ops, SparseCore 0:
  53.1 23.0 reduce-scatter.3
  90.1 31.6 all-reduce.3
